TPU v7x, 32 devices: a whole 2x2x4 slice. The times are simulated.
32 devices in a mesh: rep: 2 (over x), shard: 16 (over z, y, core).
Axes of the slice: x: 2, y: 2, z: 4, core: 2. Of those that a mesh axis runs over, the one named last changes fastest.
Arguments:
- tokens_x: bfloat16 [8192, 4096], P(('rep', 'shard')), may hold values from -6 to 6
- key_grad: bfloat16 [8192, 1024], P(('rep', 'shard')), may hold values from -0.06591797 to 0.06591797
- left_root: bfloat16 [64, 512, 512], P('shard'), may hold values from -1 to 3
- slot_grads: bfloat16 [64, 512, 512], P('shard'), may hold values from -6 to 6
- right_root: bfloat16 [64, 512, 512], P('shard'), may hold values from -1 to 3
- block_slot: int32 [32], replicated, may hold values from 0 to 63, as said below
Outputs:
- grad_key: float32 [4096, 1024], P('shard')
- update: bfloat16 [512, 32, 512], P('shard')
Inputs may be any that keep to these rules, and one draw needn't show every extreme that they name: `block_slot`: the entries are distinct; slot v is slot v % 4 of shard index v // 4; no shard index holds more than 4 blocks, and some shard index holds exactly 4.
All inputs are finite; a program needn't handle non-finite values.
Results may differ from a plain program's by a relative error of at most 0.006.
Values may be sent and summed in bfloat16 or wider, within the bound.
A program may use at most 128 MiB of HBM per device.

v0:
```python
import jax
import jax.numpy as jnp
from jax import lax
from jax.sharding import PartitionSpec as P


def column_term(features, cotangent):
    return lax.dot_general(
        features, cotangent, (((0,), (0,)), ((), ())), preferred_element_type=jnp.float32
    )


def precondition(left_block, grad_block, right_block):
    left_part = jnp.einsum(
        "sij,sjk->sik", left_block, grad_block, preferred_element_type=jnp.float32
    ).astype(jnp.bfloat16)
    return jnp.einsum(
        "sij,sjk->isk", left_part, right_block, preferred_element_type=jnp.float32
    ).astype(jnp.bfloat16)


def shards(tokens_x, key_grad, left_root, slot_grads, right_root, block_slot):
    n_shard = lax.axis_size("shard")
    n_rep = lax.axis_size("rep")
    own_rows = lax.psum_scatter(
        column_term(tokens_x, key_grad), "shard", scatter_dimension=0, tiled=True
    )
    grad_key = lax.psum(own_rows, "rep")
    slot_count = left_root.shape[0]
    half_slots = slot_count // n_rep
    first_slot = lax.axis_index("rep") * half_slots

    def own_half(values):
        return lax.dynamic_slice_in_dim(values, first_slot, half_slots, 0)

    product = precondition(own_half(left_root), own_half(slot_grads), own_half(right_root))
    received = lax.all_to_all(product, "shard", split_axis=0, concat_axis=1, tiled=True)
    joined = lax.all_gather(received, "rep", axis=1, tiled=True)
    owner = block_slot // slot_count
    within = block_slot % slot_count
    position = (
        within // half_slots * (n_shard * half_slots) + owner * half_slots + within % half_slots
    )
    update = jnp.take(joined, position, axis=1)
    return (grad_key, update)


def solution(mesh):
    return jax.shard_map(
        shards,
        mesh=mesh,
        in_specs=(
            P(("rep", "shard"), None),
            P(("rep", "shard"), None),
            P("shard", None, None),
            P("shard", None, None),
            P("shard", None, None),
            P(),
        ),
        out_specs=(P("shard", None), P("shard", None, None)),
        check_vma=False,
    )
```

profile of v0, /device:TPU:0, one launch (start us, length us, event | category | flops | bytes accessed | tf_op | source)
XLA Modules:
  0.0 247.9 jit_solution(18152596970215478150)
XLA Ops:
  8.0 0.0 copy-start
  8.0 0.0 reduce-scatter.2.cloned.1.call-start
  8.1 1.5 copy-done
  9.6 9.2 %fusion.9 = f32[4096,1024]{1,0:T(8,128)} fusion(bf16[256,4096]{1,0:T(8,128)(2,1)S(1)} %copy-done, bf16[256,1024]{1,0:T(8,128)(2,1)} %param.7), kind=kOutput, calls=%fused_computation.23 | convolution fusion | flops 2147483648 | bytes 19398656 | tf_op jit(solution)/shard_map/dot_general | solution.py:8
  18.8 0.0 reduce-scatter.2.cloned.1.call-update
  18.8 0.0 all-gather.2.cloned.1.call-start
  18.8 4.1 %fusion = bf16[512,2,512]{0,2,1:T(8,128)(2,1)} fusion(bf16[4,512,512]{2,1,0:T(8,128)(2,1)} %param.9, s32[]{:T(128)S(6)} %select_n.37, bf16[4,512,512]{2,1,0:T(8,128)(2,1)} %param.8, bf16[4,512,512]{2,1,0:T(8,128)(2,1)} %param.10), kind=kOutput, calls=%fused_computation.3 | convolution fusion | flops 1074790400 | bytes 4195840 | tf_op jit(solution)/shard_map/sij,sjk->isk/dot_general | solution.py:17
  22.9 2.5 %copy.14 = bf16[512,2,512]{2,1,0:T(2,128)(2,1)S(1)} copy(bf16[512,2,512]{0,2,1:T(8,128)(2,1)} %fusion) | data formatting | bytes 2097152 | tf_op jit(solution)/shard_map/convert_element_type | solution.py:19
  25.4 31.9 %all_to_all.18 = bf16[512,2,512]{2,1,0:T(2,128)(2,1)S(1)} all-to-all(bf16[512,2,512]{2,1,0:T(2,128)(2,1)S(1)} %copy.14), channel_id=1, replica_groups=mesh['rep'=2,'shard'=16] {'shard'}, dimensions={0} | all-to-all | bytes 2097152 | tf_op jit(solution)/shard_map/all_to_all | solution.py:37
  57.3 0.2 copy.15
  57.5 0.0 copy-start.1
  57.5 1.0 copy.16
  58.6 0.0 all-gather.2.cloned.1.call-update
  58.6 0.0 all-reduce.2.cloned.1.call-start
  58.6 140.4 %reduce-scatter.2.cloned.1.call-done = f32[256,1024]{1,0:T(8,128)} async-done(((f32[4096,1024]{1,0:T(8,128)}), f32[256,1024]{1,0:T(8,128)}) %reduce-scatter.2.cloned.1.call-update) | async-done | bytes 1048592 | tf_op jit(solution)/shard_map/reduce_scatter | solution.py:25
  199.0 0.0 all-reduce.2.cloned.1.call-update
  199.0 0.0 copy-done.1
  199.1 0.0 all-gather.2.cloned.1.call-done
  199.1 2.2 gather_fusion
  201.3 0.2 select_bitcast_fusion
  201.5 1.5 copy.17
  203.0 35.1 %all-reduce.2.cloned.1.call-done = f32[256,1024]{1,0:T(8,128)} async-done(((f32[256,1024]{1,0:T(8,128)}), f32[256,1024]{1,0:T(8,128)}) %all-reduce.2.cloned.1.call-update) | async-done | bytes 1048592 | tf_op jit(solution)/shard_map/psum | solution.py:28
  238.2 2.3 copy.20
  (2 shorter events, 0.0 us)
Async XLA Ops:
  8.0 1.6 copy-start
  8.0 191.0 %reduce-scatter.2.cloned.1.call-start = ((), (), s32[]{:S(2)}) async-start(), calls=%async_computation.2 | async-start | bytes 17825792 | tf_op jit(solution)/shard_map/reduce_scatter | solution.py:25
  18.8 180.3 %all-gather.2.cloned.1.call-start = ((), (), s32[]{:S(2)}) async-start(), calls=%async_computation.4 | async-start | bytes 3145728 | tf_op jit(solution)/shard_map/all_gather | solution.py:38
  57.5 141.5 %copy-start.1 = (s32[32]{0:T(128)S(1)}, s32[32]{0:T(128)}, u32[]{:S(2)}) copy-start(s32[32]{0:T(128)} %param.11) | copy-start | bytes 388
  58.6 179.6 %all-reduce.2.cloned.1.call-start = ((), (), s32[]{:S(2)}) async-start(), calls=%async_computation.3 | async-start | bytes 2097152 | tf_op jit(solution)/shard_map/psum | solution.py:28
Sparse Core Ops, SparseCore 0:
  18.9 180.0 reduce-scatter.1
Sparse Core Ops, SparseCore 1:
  58.7 33.3 all-gather.1
  199.1 39.0 all-reduce.1
where the time goes:
time: 248 us
  waiting for transfers between devices  176 us (71%)
  blocking collectives  31.9 us (13%)
  between operations  15.6 us (6%)
  matrix products  13.2 us (5%)
  local copies, waits for them, and re-layouts  11.3 us (5%)
    reduce_scatter x1, waiting for transfers between devices, shards(): lax.psum_scatter(column_term(tokens_x, key_grad), 'shard', scatter_dimens...  140 us
    psum x1, waiting for transfers between devices, shards(): grad_key = lax.psum(own_rows, 'rep')  35.1 us
    all_to_all x1, blocking collectives, shards(): lax.all_to_all(product, 'shard', split_axis=0, concat_axis=1, tiled=True)  31.9 us
    dot_general x1, matrix products, column_term(): lax.dot_general(features, cotangent, (((0,), (0,)), ((), ())), preferred_...  9.16 us
    unnamed x6, local copies, waits for them, and re-layouts  5.4 us
  transfers between devices with their start and end apart: 3, of which 2 were waited for; matrix products, arithmetic and copies ran while one was open for 5% of the time, Pallas kernels for 0%

commit v1 on v0

--- a/solution.py
+++ b/solution.py
@@ -1,7 +1,15 @@
+import functools
+
 import jax
 import jax.numpy as jnp
 from jax import lax
+from jax.experimental import pallas as pl
+from jax.experimental.pallas import tpu as pltpu
 from jax.sharding import PartitionSpec as P
+
+MESH = pl.DeviceIdType.MESH
+GROUP = 4
+PIECES = 4
 
 
 def column_term(features, cotangent):
@@ -19,7 +27,7 @@
     ).astype(jnp.bfloat16)
 
 
-def shards(tokens_x, key_grad, left_root, slot_grads, right_root, block_slot):
+def plain_shards(tokens_x, key_grad, left_root, slot_grads, right_root, block_slot):
     n_shard = lax.axis_size("shard")
     n_rep = lax.axis_size("rep")
     own_rows = lax.psum_scatter(
@@ -43,6 +51,282 @@
     )
     update = jnp.take(joined, position, axis=1)
     return (grad_key, update)
+
+
+def remote(src, dst, send_sem, recv_sem, axis, index):
+    return pltpu.make_async_remote_copy(
+        src_ref=src,
+        dst_ref=dst,
+        send_sem=send_sem,
+        recv_sem=recv_sem,
+        device_id={axis: index},
+        device_id_type=MESH,
+    )
+
+
+def far_first(outer):
+    return sorted(range(1, outer), key=lambda off: -min(off, outer - off)) + [0]
+
+
+def kernel(
+    n, slot_ref, x_ref, g_ref, lr_ref, sg_ref, rr_ref, og_ref, ou_ref,
+    x_all, g_all, lr, sg, rr, prod, upd, mine, theirs, part, landed, own, half_out, half_in,
+    local_sem, x_local, barrier_free, g_send, g_recv, x_send, x_recv, u_send, u_recv,
+    z_send, z_recv, r_send, r_recv, v_send, v_recv,
+):
+    me = lax.axis_index("shard")
+    rep = lax.axis_index("rep")
+    other_rep = 1 - rep
+    q = me % GROUP
+    z = me // GROUP
+    base = z * GROUP
+    outer = n // GROUP
+    q_core = q + 1 - 2 * (q % 2)
+    q_far = (q + 2) % GROUP
+    q_both = (q_core + 2) % GROUP
+    tok = x_ref.shape[0]
+    cols = x_ref.shape[1] // n
+    slots = lr_ref.shape[0]
+    blocks = slot_ref.shape[0]
+    offsets = far_first(outer)
+
+    def tokens_of(index):
+        return pl.ds(index * tok, tok)
+
+    def columns(d, index):
+        return pl.ds(pl.multiple_of((d * GROUP + index) * cols, 128), cols)
+
+    copy_lr = pltpu.make_async_copy(lr_ref.at[:, :, rep], lr, local_sem.at[0])
+    copy_sg = pltpu.make_async_copy(sg_ref, sg, local_sem.at[1])
+    copy_rr = pltpu.make_async_copy(rr_ref, rr, local_sem.at[2])
+    copy_g = pltpu.make_async_copy(g_ref, g_all.at[tokens_of(q)], local_sem.at[3])
+    copies_x = []
+    for d in range(outer):
+        copies_x.append(
+            pltpu.make_async_copy(
+                x_ref.at[:, columns(d, q)], x_all.at[d, tokens_of(q)], x_local.at[d]
+            )
+        )
+    copy_lr.start()
+    copy_sg.start()
+    copy_rr.start()
+    copy_g.start()
+    for copy in copies_x:
+        copy.start()
+
+    barrier = pltpu.get_barrier_semaphore()
+    for step in range(1, n):
+        pl.semaphore_signal(
+            barrier, inc=1, device_id={"shard": (me + step) % n}, device_id_type=MESH
+        )
+    pl.semaphore_signal(barrier, inc=1, device_id={"rep": other_rep}, device_id_type=MESH)
+    pl.semaphore_wait(barrier, n)
+
+    sent = []
+
+    def send(*args):
+        copy = remote(*args)
+        copy.start()
+        sent.append(copy)
+
+    for order, target in enumerate((q_far, q_core)):
+        send(
+            g_ref, g_all.at[tokens_of(q)], g_send.at[order], g_recv.at[q], "shard", base + target
+        )
+    for order, off in enumerate(offsets):
+        d = (z + off) % outer
+        for place, target in enumerate((q_far, q_both, q_core)):
+            send(
+                x_ref.at[:, columns(d, target)],
+                x_all.at[d, tokens_of(q)],
+                x_send.at[order, place],
+                x_recv.at[q, d],
+                "shard",
+                base + target,
+            )
+
+    copy_lr.wait()
+    copy_sg.wait()
+    copy_rr.wait()
+    height = lr.shape[2]
+    width = lr.shape[3]
+    for s in range(slots):
+        left = jnp.dot(
+            lr[s].reshape(n * height, width), sg[s], preferred_element_type=jnp.float32
+        ).astype(jnp.bfloat16)
+        both = jnp.dot(left, rr[s], preferred_element_type=jnp.float32).astype(jnp.bfloat16)
+        prod[:, s] = both.reshape(n, height, width)
+    for step in range(1, n):
+        target = (me + step) % n
+        send(
+            prod.at[target],
+            upd.at[pl.ds(me * slots, slots)],
+            u_send.at[step],
+            u_recv.at[me],
+            "shard",
+            target,
+        )
+    upd[pl.ds(me * slots, slots)] = prod[me]
+
+    def arrive(dst, recv_sem):
+        remote(dst, dst, barrier_free, recv_sem, "shard", (me + 1) % n).wait_recv()
+
+    arrive(g_all.at[tokens_of(q_far)], g_recv.at[q_far])
+    send(
+        g_all.at[tokens_of(q_far)],
+        g_all.at[tokens_of(q_far)],
+        g_send.at[2],
+        g_recv.at[q_far],
+        "shard",
+        base + q_core,
+    )
+    copy_g.wait()
+    arrive(g_all.at[tokens_of(q_core)], g_recv.at[q_core])
+    arrive(g_all.at[tokens_of(q_both)], g_recv.at[q_both])
+    for copy in copies_x:
+        copy.wait()
+
+    piece = own.shape[2]
+    for order, off in enumerate(offsets):
+        d = (z + off) % outer
+        for source in (q_core, q_far, q_both):
+            arrive(x_all.at[d, tokens_of(source)], x_recv.at[source, d])
+        for p in range(PIECES):
+            value = lax.dot_general(
+                x_all[d],
+                g_all[:, p * piece : (p + 1) * piece],
+                (((0,), (0,)), ((), ())),
+                preferred_element_type=jnp.float32,
+            )
+            if off == 0:
+                own[p] = value
+            else:
+                part[order, p] = value.astype(jnp.bfloat16)
+                send(
+                    part.at[order, p],
+                    landed.at[z, p],
+                    z_send.at[order, p],
+                    z_recv.at[z, p],
+                    "shard",
+                    d * GROUP + q,
+                )
+
+    for step in range(1, n):
+        source = (me + n - step) % n
+        arrive(upd.at[pl.ds(source * slots, slots)], u_recv.at[source])
+
+    def pick(b, carry):
+        mine[b] = upd[slot_ref[b]]
+        return carry
+
+    lax.fori_loop(0, blocks, pick, 0)
+    send(mine, theirs, v_send, v_recv, "rep", other_rep)
+    ou_ref[rep] = mine[...]
+
+    for p in range(PIECES):
+        total = own[p]
+        for off in offsets[:-1]:
+            source = (z + outer - off) % outer
+            arrive(landed.at[source, p], z_recv.at[source, p])
+            total = total + landed[source, p].astype(jnp.float32)
+        half_out[p] = total.astype(jnp.bfloat16)
+        send(half_out.at[p], half_in.at[p], r_send.at[p], r_recv.at[p], "rep", other_rep)
+
+    arrive(theirs, v_recv)
+    ou_ref[other_rep] = theirs[...]
+    for p in range(PIECES):
+        arrive(half_in.at[p], r_recv.at[p])
+        og_ref[:, p * piece : (p + 1) * piece] = half_out[p].astype(jnp.float32) + half_in[
+            p
+        ].astype(jnp.float32)
+    for copy in sent:
+        copy.wait_send()
+
+
+def fused_shards(tokens_x, key_grad, left_root, slot_grads, right_root, block_slot):
+    n = lax.axis_size("shard")
+    n_rep = lax.axis_size("rep")
+    outer = n // GROUP
+    tok, d_model = tokens_x.shape
+    key_width = key_grad.shape[1]
+    cols = d_model // n
+    slots, order_b, width = left_root.shape
+    height = order_b // n // n_rep
+    blocks = block_slot.shape[0]
+    piece = key_width // PIECES
+    bf16, f32 = jnp.bfloat16, jnp.float32
+    dma = pltpu.SemaphoreType.DMA
+    any_spec = pl.BlockSpec(memory_space=pl.ANY)
+    vmem_spec = pl.BlockSpec(memory_space=pltpu.VMEM)
+    grad_key, rows = pl.pallas_call(
+        functools.partial(kernel, n),
+        out_shape=(
+            jax.ShapeDtypeStruct((cols, key_width), f32),
+            jax.ShapeDtypeStruct((n_rep, blocks, height, width), bf16),
+        ),
+        in_specs=[pl.BlockSpec(memory_space=pltpu.SMEM)] + [any_spec] * 5,
+        out_specs=(vmem_spec, vmem_spec),
+        scratch_shapes=[
+            pltpu.VMEM((outer, GROUP * tok, cols), bf16),
+            pltpu.VMEM((GROUP * tok, key_width), bf16),
+            pltpu.VMEM((slots, n, height, width), bf16),
+            pltpu.VMEM(slot_grads.shape, bf16),
+            pltpu.VMEM(right_root.shape, bf16),
+            pltpu.VMEM((n, slots, height, width), bf16),
+            pltpu.VMEM((n * slots, height, width), bf16),
+            pltpu.VMEM((blocks, height, width), bf16),
+            pltpu.VMEM((blocks, height, width), bf16),
+            pltpu.VMEM((outer - 1, PIECES, cols, piece), bf16),
+            pltpu.VMEM((outer, PIECES, cols, piece), bf16),
+            pltpu.VMEM((PIECES, cols, piece), f32),
+            pltpu.VMEM((PIECES, cols, piece), bf16),
+            pltpu.VMEM((PIECES, cols, piece), bf16),
+            dma((4,)),
+            dma((outer,)),
+            dma,
+            dma((3,)),
+            dma((GROUP,)),
+            dma((outer, 3)),
+            dma((GROUP, outer)),
+            dma((n,)),
+            dma((n,)),
+            dma((outer - 1, PIECES)),
+            dma((outer, PIECES)),
+            dma((PIECES,)),
+            dma((PIECES,)),
+            dma,
+            dma,
+        ],
+        compiler_params=pltpu.CompilerParams(
+            collective_id=0, has_side_effects=True, vmem_limit_bytes=60 * 1024 * 1024
+        ),
+    )(
+        block_slot,
+        tokens_x,
+        key_grad,
+        left_root.reshape(slots, n, n_rep, height, width),
+        slot_grads,
+        right_root,
+    )
+    update = jnp.transpose(rows, (0, 2, 1, 3)).reshape(n_rep * height, blocks, width)
+    return (grad_key, update)
+
+
+def shards(tokens_x, key_grad, left_root, slot_grads, right_root, block_slot):
+    n = lax.axis_size("shard")
+    n_rep = lax.axis_size("rep")
+    aligned = (
+        n_rep == 2
+        and n % GROUP == 0
+        and n > GROUP
+        and tokens_x.shape[1] % (n * 128) == 0
+        and key_grad.shape[1] % (PIECES * 128) == 0
+        and tokens_x.shape[0] % 16 == 0
+        and left_root.shape[1] % (n * n_rep * 16) == 0
+        and left_root.shape[2] % 128 == 0
+    )
+    program = fused_shards if aligned else plain_shards
+    return program(tokens_x, key_grad, left_root, slot_grads, right_root, block_slot)
 
 
 def solution(mesh):

time: 248 us -> 92.9 us (0.37)
  waiting for transfers between devices: 176 us -> 0 us
  Pallas kernels: 0 us -> 88.3 us
  blocking collectives: 31.9 us -> 0 us
  between operations: 15.6 us -> 0.65 us
  matrix products: 13.2 us -> 0 us
  local copies, waits for them, and re-layouts: 11.3 us -> 3.84 us
    reduce_scatter x1 -> x0, waiting for transfers between devices: 140 us -> none  [shards(): lax.psum_scatter(column_term(tokens_x, key_grad), 'shard', scatter_dimens...]
    pallas_call x0 -> x1, Pallas kernels: none -> 88.3 us  [fused_shards(): pl.pallas_call(functools.partial(kernel, n), out_shape=(jax.ShapeDtypeStr...]
    psum x1 -> x0, waiting for transfers between devices: 35.1 us -> none  [shards(): grad_key = lax.psum(own_rows, 'rep')]
    all_to_all x1 -> x0, blocking collectives: 31.9 us -> none  [shards(): lax.all_to_all(product, 'shard', split_axis=0, concat_axis=1, tiled=True)]
    dot_general x2 -> x0, matrix products: 13.2 us -> none  [the longest x1 9.16 us: column_term(): lax.dot_general(features, cotangent, (((0,), (0,)), ((), ())), preferred_...]
    unnamed x6 -> x3, local copies, waits for them, and re-layouts: 5.4 us -> 0.97 us
    transpose x0 -> x1, local copies, waits for them, and re-layouts: none -> 2.86 us  [fused_shards(): jnp.transpose(rows, (0, 2, 1, 3)).reshape(n_rep * height, blocks, width)]
    convert_element_type x1 -> x0, local copies, waits for them, and re-layouts: 2.5 us -> none  [precondition(): return jnp.einsum('sij,sjk->isk', left_part, right_block, preferred_eleme...]
  transfers between devices with their start and end apart: 3 -> 0, of which waited for: 2 -> 0; matrix products, arithmetic and copies ran while one was open for 5% -> 0% of each run, Pallas kernels for 0% -> 0%
where the time goes in v1:
time: 92.9 us; the launch traced here: 92.8 us
  Pallas kernels  88.3 us (95%)
  local copies, waits for them, and re-layouts  3.84 us (4%)
    pallas_call x1, Pallas kernels, fused_shards(): pl.pallas_call(functools.partial(kernel, n), out_shape=(jax.ShapeDtypeStr...  88.3 us
    transpose x1, local copies, waits for them, and re-layouts, fused_shards(): jnp.transpose(rows, (0, 2, 1, 3)).reshape(n_rep * height, blocks, width)  2.86 us

profile of v1, /device:TPU:0, one launch (start us, length us, event | category | flops | bytes accessed | tf_op | source)
XLA Modules:
  0.0 92.8 jit_solution(10541750307051610685)
XLA Ops:
  0.6 88.3 %shard_map.77 = (f32[256,1024]{1,0:T(8,128)}, bf16[2,32,16,512]{3,2,1,0:T(8,128)(2,1)}) custom-call(s32[32]{0:T(128)} %slot_ref.1, bf16[256,4096]{1,0:T(8,128)(2,1)} %x_ref.1, bf16[256,1024]{1,0:T(8,128)(2,1)} %g_ref.1, bf16[4,16,2,16,512]{4,3,2,1,0:T(8,128)(2,1)} %bitcast.3, bf16[4,512,512]{2,1,0:T(8,128)(2,1)} %sg_ref.1, bf16[4,512,512]{2,1,0:T(8,128)(2,1)} %rr_ref.1), custom_call_target="tpu_custom_call" | custom-call | tf_op jit(solution)/shard_map/pallas_call | solution.py:261
  88.9 0.0 copy-start
  88.9 2.9 %copy.8 = bf16[2,16,32,512]{3,2,1,0:T(8,128)(2,1)} copy(bf16[2,16,32,512]{3,1,2,0:T(8,128)(2,1)} %bitcast.5) | data formatting | bytes 2097152 | tf_op jit(solution)/shard_map/transpose | solution.py:311
  91.8 0.0 copy-done
  91.8 1.0 %copy.10 = f32[256,1024]{1,0:T(8,128)} copy(f32[256,1024]{1,0:T(8,128)S(1)} %copy-done) | data formatting | bytes 2097152
Async XLA Ops:
  88.9 2.9 %copy-start = (f32[256,1024]{1,0:T(8,128)S(1)}, f32[256,1024]{1,0:T(8,128)}, u32[]{:S(2)}) copy-start(f32[256,1024]{1,0:T(8,128)} %get-tuple-element.8) | copy-start | bytes 3145732

commit v2 on v1

--- a/solution.py
+++ b/solution.py
@@ -9,7 +9,7 @@
 
 MESH = pl.DeviceIdType.MESH
 GROUP = 4
-PIECES = 4
+PIECES = 2
 
 
 def column_term(features, cotangent):
@@ -70,9 +70,9 @@
 
 def kernel(
     n, slot_ref, x_ref, g_ref, lr_ref, sg_ref, rr_ref, og_ref, ou_ref,
-    x_all, g_all, lr, sg, rr, prod, upd, mine, theirs, part, landed, own, half_out, half_in,
+    x_all, g_all, lr, sg, rr, prod, upd, mine, theirs, part, met, kept, passed, landed, half_out, half_in,
     local_sem, x_local, barrier_free, g_send, g_recv, x_send, x_recv, u_send, u_recv,
-    z_send, z_recv, r_send, r_recv, v_send, v_recv,
+    a_send, a_recv, z_send, z_recv, r_send, r_recv, v_send, v_recv,
 ):
     me = lax.axis_index("shard")
     rep = lax.axis_index("rep")
@@ -186,30 +186,60 @@
     for copy in copies_x:
         copy.wait()
 
-    piece = own.shape[2]
+    piece = kept.shape[3]
+    half = PIECES * piece
+
+    def partial(d, side):
+        start = pl.multiple_of(side * half, 128)
+        return lax.dot_general(
+            x_all[d],
+            g_all[:, pl.ds(start, half)],
+            (((0,), (0,)), ((), ())),
+            preferred_element_type=jnp.float32,
+        )
+
+    def place_of(side, p):
+        return pl.ds(pl.multiple_of(side * half + p * piece, 128), piece)
+
+    def pass_on(order):
+        off = offsets[order]
+        for p in range(PIECES):
+            arrive(met.at[order, p], a_recv.at[order, p])
+            total = kept[order, p] + met[order, p].astype(jnp.float32)
+            if off == 0:
+                kept[order, p] = total
+            else:
+                passed[order, p] = total.astype(jnp.bfloat16)
+                send(
+                    passed.at[order, p],
+                    landed.at[z, p],
+                    z_send.at[order, p],
+                    z_recv.at[z, p],
+                    "shard",
+                    (z + off) % outer * GROUP + q,
+                )
+
     for order, off in enumerate(offsets):
         d = (z + off) % outer
         for source in (q_core, q_far, q_both):
             arrive(x_all.at[d, tokens_of(source)], x_recv.at[source, d])
+        value = partial(d, other_rep)
         for p in range(PIECES):
-            value = lax.dot_general(
-                x_all[d],
-                g_all[:, p * piece : (p + 1) * piece],
-                (((0,), (0,)), ((), ())),
-                preferred_element_type=jnp.float32,
+            part[order, p] = value[:, p * piece : (p + 1) * piece].astype(jnp.bfloat16)
+            send(
+                part.at[order, p],
+                met.at[order, p],
+                a_send.at[order, p],
+                a_recv.at[order, p],
+                "rep",
+                other_rep,
             )
-            if off == 0:
-                own[p] = value
-            else:
-                part[order, p] = value.astype(jnp.bfloat16)
-                send(
-                    part.at[order, p],
-                    landed.at[z, p],
-                    z_send.at[order, p],
-                    z_recv.at[z, p],
-                    "shard",
-                    d * GROUP + q,
-                )
+        value = partial(d, rep)
+        for p in range(PIECES):
+            kept[order, p] = value[:, p * piece : (p + 1) * piece]
+        if order > 0:
+            pass_on(order - 1)
+    pass_on(outer - 1)
 
     for step in range(1, n):
         source = (me + n - step) % n
@@ -224,7 +254,7 @@
     ou_ref[rep] = mine[...]
 
     for p in range(PIECES):
-        total = own[p]
+        total = kept[outer - 1, p]
         for off in offsets[:-1]:
             source = (z + outer - off) % outer
             arrive(landed.at[source, p], z_recv.at[source, p])
@@ -232,13 +262,13 @@
         half_out[p] = total.astype(jnp.bfloat16)
         send(half_out.at[p], half_in.at[p], r_send.at[p], r_recv.at[p], "rep", other_rep)
 
+    for p in range(PIECES):
+        og_ref[:, place_of(rep, p)] = half_out[p]
     arrive(theirs, v_recv)
     ou_ref[other_rep] = theirs[...]
     for p in range(PIECES):
         arrive(half_in.at[p], r_recv.at[p])
-        og_ref[:, p * piece : (p + 1) * piece] = half_out[p].astype(jnp.float32) + half_in[
-            p
-        ].astype(jnp.float32)
+        og_ref[:, place_of(other_rep, p)] = half_in[p]
     for copy in sent:
         copy.wait_send()
 
@@ -253,15 +283,15 @@
     slots, order_b, width = left_root.shape
     height = order_b // n // n_rep
     blocks = block_slot.shape[0]
-    piece = key_width // PIECES
+    piece = key_width // n_rep // PIECES
     bf16, f32 = jnp.bfloat16, jnp.float32
     dma = pltpu.SemaphoreType.DMA
     any_spec = pl.BlockSpec(memory_space=pl.ANY)
     vmem_spec = pl.BlockSpec(memory_space=pltpu.VMEM)
-    grad_key, rows = pl.pallas_call(
+    sums, rows = pl.pallas_call(
         functools.partial(kernel, n),
         out_shape=(
-            jax.ShapeDtypeStruct((cols, key_width), f32),
+            jax.ShapeDtypeStruct((cols, key_width), bf16),
             jax.ShapeDtypeStruct((n_rep, blocks, height, width), bf16),
         ),
         in_specs=[pl.BlockSpec(memory_space=pltpu.SMEM)] + [any_spec] * 5,
@@ -276,9 +306,11 @@
             pltpu.VMEM((n * slots, height, width), bf16),
             pltpu.VMEM((blocks, height, width), bf16),
             pltpu.VMEM((blocks, height, width), bf16),
+            pltpu.VMEM((outer, PIECES, cols, piece), bf16),
+            pltpu.VMEM((outer, PIECES, cols, piece), bf16),
+            pltpu.VMEM((outer, PIECES, cols, piece), f32),
             pltpu.VMEM((outer - 1, PIECES, cols, piece), bf16),
             pltpu.VMEM((outer, PIECES, cols, piece), bf16),
-            pltpu.VMEM((PIECES, cols, piece), f32),
             pltpu.VMEM((PIECES, cols, piece), bf16),
             pltpu.VMEM((PIECES, cols, piece), bf16),
             dma((4,)),
@@ -290,6 +322,8 @@
             dma((GROUP, outer)),
             dma((n,)),
             dma((n,)),
+            dma((outer, PIECES)),
+            dma((outer, PIECES)),
             dma((outer - 1, PIECES)),
             dma((outer, PIECES)),
             dma((PIECES,)),
@@ -308,6 +342,7 @@
         slot_grads,
         right_root,
     )
+    grad_key = sums.astype(f32)
     update = jnp.transpose(rows, (0, 2, 1, 3)).reshape(n_rep * height, blocks, width)
     return (grad_key, update)
 
@@ -320,7 +355,7 @@
         and n % GROUP == 0
         and n > GROUP
         and tokens_x.shape[1] % (n * 128) == 0
-        and key_grad.shape[1] % (PIECES * 128) == 0
+        and key_grad.shape[1] % (n_rep * PIECES * 128) == 0
         and tokens_x.shape[0] % 16 == 0
         and left_root.shape[1] % (n * n_rep * 16) == 0
         and left_root.shape[2] % 128 == 0

time: 92.9 us -> 84.9 us (0.914)
  Pallas kernels: 88.3 us -> 80.2 us
  other arithmetic: 0 us -> 1.09 us
  local copies, waits for them, and re-layouts: 3.84 us -> 2.84 us
    pallas_call x1, Pallas kernels: 88.3 us -> 80.2 us  [fused_shards(): pl.pallas_call(functools.partial(kernel, n), out_shape=(jax.ShapeDtypeStr...]
    convert_element_type x0 -> x1, other arithmetic: none -> 1.09 us  [fused_shards(): grad_key = sums.astype(f32)]
    unnamed x3 -> x2, local copies, waits for them, and re-layouts: 0.97 us -> 0.01 us
where the time goes in v2:
time: 84.9 us; the launch traced here: 84.7 us
  Pallas kernels  80.2 us (94%)
  local copies, waits for them, and re-layouts  2.84 us (3%)
  other arithmetic  1.09 us (1%)
    pallas_call x1, Pallas kernels, fused_shards(): pl.pallas_call(functools.partial(kernel, n), out_shape=(jax.ShapeDtypeStr...  80.2 us
    transpose x1, local copies, waits for them, and re-layouts, fused_shards(): jnp.transpose(rows, (0, 2, 1, 3)).reshape(n_rep * height, blocks, width)  2.83 us

profile of v2, /device:TPU:0, one launch (start us, length us, event | category | flops | bytes accessed | tf_op | source)
XLA Modules:
  0.0 84.7 jit_solution(18036290338881226330)
XLA Ops:
  0.6 80.2 %shard_map.77 = (bf16[256,1024]{1,0:T(8,128)(2,1)}, bf16[2,32,16,512]{3,2,1,0:T(8,128)(2,1)}) custom-call(s32[32]{0:T(128)} %slot_ref.1, bf16[256,4096]{1,0:T(8,128)(2,1)} %x_ref.1, bf16[256,1024]{1,0:T(8,128)(2,1)} %g_ref.1, bf16[4,16,2,16,512]{4,3,2,1,0:T(8,128)(2,1)} %bitcast.3, bf16[4,512,512]{2,1,0:T(8,128)(2,1)} %sg_ref.1, bf16[4,512,512]{2,1,0:T(8,128)(2,1)} %rr_ref.1), custom_call_target="tpu_custom_call" | custom-call | tf_op jit(solution)/shard_map/pallas_call | solution.py:291
  80.8 0.0 copy-start
  80.8 2.8 %copy.8 = bf16[2,16,32,512]{3,2,1,0:T(8,128)(2,1)} copy(bf16[2,16,32,512]{3,1,2,0:T(8,128)(2,1)} %bitcast.5) | data formatting | bytes 2097152 | tf_op jit(solution)/shard_map/transpose | solution.py:346
  83.6 0.0 copy-done
  83.6 1.1 %convert_element_type.3 = f32[256,1024]{1,0:T(8,128)} convert(bf16[256,1024]{1,0:T(8,128)(2,1)S(1)} %copy-done) | non-fusion elementwise | flops 262144 | bytes 1572864 | tf_op jit(solution)/shard_map/convert_element_type | solution.py:345
Async XLA Ops:
  80.8 2.8 %copy-start = (bf16[256,1024]{1,0:T(8,128)(2,1)S(1)}, bf16[256,1024]{1,0:T(8,128)(2,1)}, u32[]{:S(2)}) copy-start(bf16[256,1024]{1,0:T(8,128)(2,1)} %get-tuple-element.4) | copy-start | bytes 1572868

commit v3 on v2

--- a/solution.py
+++ b/solution.py
@@ -241,18 +241,6 @@
             pass_on(order - 1)
     pass_on(outer - 1)
 
-    for step in range(1, n):
-        source = (me + n - step) % n
-        arrive(upd.at[pl.ds(source * slots, slots)], u_recv.at[source])
-
-    def pick(b, carry):
-        mine[b] = upd[slot_ref[b]]
-        return carry
-
-    lax.fori_loop(0, blocks, pick, 0)
-    send(mine, theirs, v_send, v_recv, "rep", other_rep)
-    ou_ref[rep] = mine[...]
-
     for p in range(PIECES):
         total = kept[outer - 1, p]
         for off in offsets[:-1]:
@@ -261,6 +249,18 @@
             total = total + landed[source, p].astype(jnp.float32)
         half_out[p] = total.astype(jnp.bfloat16)
         send(half_out.at[p], half_in.at[p], r_send.at[p], r_recv.at[p], "rep", other_rep)
+
+    for step in range(1, n):
+        source = (me + n - step) % n
+        arrive(upd.at[pl.ds(source * slots, slots)], u_recv.at[source])
+
+    def pick(b, carry):
+        mine[b] = upd[slot_ref[b]]
+        return carry
+
+    lax.fori_loop(0, blocks, pick, 0)
+    send(mine, theirs, v_send, v_recv, "rep", other_rep)
+    ou_ref[rep] = mine[...]
 
     for p in range(PIECES):
         og_ref[:, place_of(rep, p)] = half_out[p]

time: 84.9 us -> 87.8 us (1.034)
  Pallas kernels: 80.2 us -> 83.1 us
    pallas_call x1, Pallas kernels: 80.2 us -> 83.1 us  [fused_shards(): pl.pallas_call(functools.partial(kernel, n), out_shape=(jax.ShapeDtypeStr...]
where the time goes in v3:
time: 87.8 us; the launch traced here: 87.6 us
  Pallas kernels  83.1 us (95%)
  local copies, waits for them, and re-layouts  2.84 us (3%)
  other arithmetic  1.09 us (1%)
    pallas_call x1, Pallas kernels, fused_shards(): pl.pallas_call(functools.partial(kernel, n), out_shape=(jax.ShapeDtypeStr...  83.1 us
    transpose x1, local copies, waits for them, and re-layouts, fused_shards(): jnp.transpose(rows, (0, 2, 1, 3)).reshape(n_rep * height, blocks, width)  2.83 us

profile of v3, /device:TPU:0, one launch (start us, length us, event | category | flops | bytes accessed | tf_op | source)
XLA Modules:
  0.0 87.6 jit_solution(11870491719468731011)
XLA Ops:
  0.6 83.1 %shard_map.77 = (bf16[256,1024]{1,0:T(8,128)(2,1)}, bf16[2,32,16,512]{3,2,1,0:T(8,128)(2,1)}) custom-call(s32[32]{0:T(128)} %slot_ref.1, bf16[256,4096]{1,0:T(8,128)(2,1)} %x_ref.1, bf16[256,1024]{1,0:T(8,128)(2,1)} %g_ref.1, bf16[4,16,2,16,512]{4,3,2,1,0:T(8,128)(2,1)} %bitcast.3, bf16[4,512,512]{2,1,0:T(8,128)(2,1)} %sg_ref.1, bf16[4,512,512]{2,1,0:T(8,128)(2,1)} %rr_ref.1), custom_call_target="tpu_custom_call" | custom-call | tf_op jit(solution)/shard_map/pallas_call | solution.py:291
  83.7 0.0 copy-start
  83.7 2.8 %copy.8 = bf16[2,16,32,512]{3,2,1,0:T(8,128)(2,1)} copy(bf16[2,16,32,512]{3,1,2,0:T(8,128)(2,1)} %bitcast.5) | data formatting | bytes 2097152 | tf_op jit(solution)/shard_map/transpose | solution.py:346
  86.5 0.0 copy-done
  86.5 1.1 %convert_element_type.3 = f32[256,1024]{1,0:T(8,128)} convert(bf16[256,1024]{1,0:T(8,128)(2,1)S(1)} %copy-done) | non-fusion elementwise | flops 262144 | bytes 1572864 | tf_op jit(solution)/shard_map/convert_element_type | solution.py:345
Async XLA Ops:
  83.7 2.8 %copy-start = (bf16[256,1024]{1,0:T(8,128)(2,1)S(1)}, bf16[256,1024]{1,0:T(8,128)(2,1)}, u32[]{:S(2)}) copy-start(bf16[256,1024]{1,0:T(8,128)(2,1)} %get-tuple-element.4) | copy-start | bytes 1572868
